TPU v7x, 128 devices: a whole 4x4x4 slice. The times are simulated.
128 devices in a mesh: psg: 16 (over x_hi, y, core), qry: 8 (over z, x_lo).
Axes of the slice: x: 4 (x_hi: 2, x_lo: 2; x = x_hi * 2 + x_lo), y: 4, z: 4, core: 2. Of those that a mesh axis runs over, the one named last changes fastest.
Arguments:
- hidden: bfloat16 [1024, 4096], P('qry'), may hold values from -6 to 6
- norm_gain: float32 [4096], replicated, may hold values from 0.5 to 1.5
- proj_weight: bfloat16 [4096, 4096], P('psg', 'qry'), may hold values from -0.09375 to 0.09375
- pq_codes: int32 [32768, 512], P('psg', 'qry'), may hold values from 0 to 255
- codebook: bfloat16 [512, 8, 256], P('qry'), may hold values from -560 to 560
- positives: int32 [1024], replicated, may hold values from 0 to 32767
Outputs:
- losses: float32 [1024], P('qry')
- hidden_grad: bfloat16 [1024, 4096], P('qry')
- weight_grad: float32 [4096, 4096], P('psg', 'qry')
- codebook_grad: float32 [512, 8, 256], P('qry')
All inputs are finite; a program needn't handle non-finite values.
Results may differ from a plain program's by a relative error of at most 0.019.
The roundings to bfloat16 on the way count: a program that leaves them out, or rounds other values in their place, can miss the bound.
Values may be sent and summed in bfloat16 or wider, within the bound.
A program may use at most 128 MiB of HBM per device.

v0:
```python
import jax
import jax.numpy as jnp
from jax import lax
from jax.sharding import Mesh
from jax.sharding import PartitionSpec as P

QRY = ("qry_0", "qry_1")
score_scale = 0.0625
norm_eps = 1e-06


def summed_rows(x, axes, dim):
    if not axes:
        return x
    nearer = lax.psum_scatter(x, axes[0], scatter_dimension=dim, tiled=True)
    return summed_rows(nearer, axes[1:], dim)


def sent_to_all(x, axis):
    copies = jnp.broadcast_to(x, (lax.axis_size(axis), *x.shape))
    return lax.all_to_all(copies, axis, split_axis=0, concat_axis=0, tiled=True)


def gathered_once(x, axis):
    leaves = jax.tree.leaves(x)
    turns = sorted(range(len(leaves)), key=lambda k: -leaves[k].size)
    width = (1, *leaves[turns[0]].shape)[-1]
    lines = [
        jnp.pad(leaves[k].reshape(-1), (0, -leaves[k].size % width)).reshape(-1, width)
        for k in turns
    ]
    both, at, found = (sent_to_all(jnp.concatenate(lines), axis), 0, {})
    for k, line in zip(turns, lines):
        piece = both[:, at : at + len(line)].reshape(len(both), -1)
        found[k] = piece[:, : leaves[k].size].reshape(-1, *leaves[k].shape)
        at += len(line)
    numbers = iter(range(len(leaves)))
    return jax.tree.map(lambda _: found[next(numbers)], x)


def folded_in_pairs(pieces, combine):
    while len(jax.tree.leaves(pieces)[0]) > 1:
        pieces = jax.vmap(combine)(
            *(jax.tree.map(lambda part: part[side::2], pieces) for side in (0, 1))
        )
    return jax.tree.map(lambda part: part[0], pieces)


def joined_all(x, axis, combine):
    pieces = gathered_once(x, axis)
    return folded_in_pairs(pieces, combine)


def code_hot(code_block, book):
    levels = lax.broadcasted_iota(jnp.int32, code_block.shape + (book.shape[2],), 2)
    return (code_block[:, :, None] == levels).astype(jnp.bfloat16)


def per_device(hidden, norm_gain, proj_weight, pq_codes, codebook, positives):
    gathered = lax.all_gather(hidden, QRY, axis=0, tiled=True)
    floats_all = gathered.astype(jnp.float32)
    inverse_all = lax.rsqrt(jnp.mean(floats_all * floats_all, axis=1, keepdims=True) + norm_eps)
    normed = (floats_all * inverse_all * norm_gain[None, :]).astype(jnp.bfloat16)
    columns = proj_weight.shape[1]
    whole_weight = lax.all_gather(proj_weight, "psg", axis=0, tiled=True)
    query_float = jnp.dot(normed, whole_weight, preferred_element_type=jnp.float32)
    queries = query_float.astype(jnp.bfloat16)
    passage_count = pq_codes.shape[0]
    sub_count = codebook.shape[0]
    sub_width = codebook.shape[1]
    block_rows = min(passage_count, 512)
    code_blocks = pq_codes.reshape(passage_count // block_rows, block_rows, sub_count)

    def decode(code_block):
        hot_table = code_hot(code_block, codebook)
        vectors = jnp.einsum(
            "pmk,mdk->pmd", hot_table, codebook, preferred_element_type=jnp.float32
        )
        return vectors.astype(jnp.bfloat16).reshape(block_rows, columns)

    passages = lax.map(decode, code_blocks).reshape(passage_count, columns)
    partial_value = (
        lax.dot_general(
            queries, passages, (((1,), (1,)), ((), ())), preferred_element_type=jnp.float32
        )
        * score_scale
    )
    qry_index = lax.axis_index(QRY)
    own_rows = hidden.shape[0]
    scores = summed_rows(partial_value, QRY, 0)
    row_targets = lax.dynamic_slice_in_dim(positives, qry_index * own_rows, own_rows, 0)
    local_target = row_targets - lax.axis_index("psg") * passage_count
    target = lax.broadcasted_iota(jnp.int32, scores.shape, 1) == local_target[:, None]
    local_max = jnp.max(scores, axis=1)
    positive_part = jnp.sum(jnp.where(target, scores, 0.0), axis=1)
    local_total = jnp.sum(jnp.exp(scores - local_max[:, None]), axis=1)

    def combine(first, second):
        higher = jnp.maximum(first[0], second[0])
        joined = first[1] * jnp.exp(first[0] - higher) + second[1] * jnp.exp(second[0] - higher)
        return (higher, joined, first[2] + second[2])

    row_max, row_total, positive_score = joined_all(
        (local_max, local_total, positive_part), "psg", combine
    )
    losses = jnp.log(row_total) + row_max - positive_score
    score_grad = (
        jnp.exp(scores - row_max[:, None]) / row_total[:, None] - target.astype(jnp.float32)
    ).astype(jnp.bfloat16)
    all_grad = lax.all_gather(score_grad, QRY, axis=0, tiled=True)
    query_part = jnp.dot(all_grad, passages, preferred_element_type=jnp.float32) * score_scale
    query_grad = lax.psum(query_part, "psg").astype(jnp.bfloat16)
    passage_grad = (
        lax.dot_general(
            all_grad, queries, (((0,), (0,)), ((), ())), preferred_element_type=jnp.float32
        )
        * score_scale
    ).astype(jnp.bfloat16)
    grad_blocks = passage_grad.reshape(
        passage_count // block_rows, block_rows, sub_count, sub_width
    )

    def add_book(carry, paired):
        code_block, grad_block = paired
        hot_table = code_hot(code_block, codebook)
        return (
            carry
            + jnp.einsum("pmk,pmd->mdk", hot_table, grad_block, preferred_element_type=jnp.float32),
            None,
        )

    book_part, unused = lax.scan(
        add_book, jnp.zeros(codebook.shape, jnp.float32), (code_blocks, grad_blocks)
    )
    codebook_grad = lax.psum(book_part.astype(jnp.bfloat16), "psg").astype(jnp.float32)
    row_span = proj_weight.shape[0]
    normed_rows = lax.dynamic_slice_in_dim(normed, lax.axis_index("psg") * row_span, row_span, 1)
    weight_grad = lax.dot_general(
        normed_rows, query_grad, (((0,), (0,)), ((), ())), preferred_element_type=jnp.float32
    )
    norm_part = lax.dot_general(
        query_grad, whole_weight, (((1,), (1,)), ((), ())), preferred_element_type=jnp.float32
    )
    norm_back = lax.psum_scatter(
        norm_part.astype(jnp.bfloat16), QRY, scatter_dimension=0, tiled=True
    ).astype(jnp.float32)
    floats_own = hidden.astype(jnp.float32)
    inverse_own = lax.rsqrt(jnp.mean(floats_own * floats_own, axis=1, keepdims=True) + norm_eps)
    scaled = norm_back * norm_gain[None, :]
    hidden_grad = (
        inverse_own * scaled
        - floats_own
        * inverse_own
        * inverse_own
        * inverse_own
        * jnp.mean(scaled * floats_own, axis=1, keepdims=True)
    ).astype(jnp.bfloat16)
    return (losses, hidden_grad, weight_grad, codebook_grad)


def solution(mesh):
    split = Mesh(mesh.devices.reshape(mesh.shape["psg"], 4, 2), ("psg", "qry_0", "qry_1"))
    return jax.shard_map(
        per_device,
        mesh=split,
        in_specs=(P(QRY, None), P(), P("psg", QRY), P("psg", QRY), P(QRY, None, None), P()),
        out_specs=(P(QRY), P(QRY, None), P("psg", QRY), P(QRY, None, None)),
        check_vma=False,
    )
```

profile of v0, /device:TPU:1, one launch (start us, length us, event | category | flops | bytes accessed | tf_op | source)
XLA Modules:
  0.0 852.5 jit_solution(15345686447529952865)
XLA Ops:
  7.2 0.7 all-gather.4.cloned.1.call-update
  7.9 0.7 all-gather.6.cloned.1.call-update
  8.7 1.1 copy.27
  9.8 33.1 %while.21 = (s32[]{:T(128)}, bf16[4,512,512]{2,1,0:T(8,128)(2,1)}, s32[4,512,64]{1,2,0:T(8,128)S(1)}, bf16[64,8,256]{2,1,0:T(8,128)(2,1)}, s32[]{:T(128)}) while((s32[]{:T(128)}, bf16[4,512,512]{2,1,0:T(8,128)(2,1)}, s32[4,512,64]{1,2,0:T(8,128)S(1)}, bf16[64,8,256]{2,1,0:T(8,128)(2,1)}, s32[]{:T(128)}) %tuple.74), condition=%wide.region_2.3_spmd, body=%wide.region_1.2_spmd.sunk | while | flops 142868480 | bytes 3277377 | solution.py:81
  9.8 7.2 fusion.43
  17.0 0.2 copy.29
  17.2 0.8 constant_dynamic-update-slice_fusion.2
  18.1 7.2 fusion.43
  25.5 0.9 constant_dynamic-update-slice_fusion.2
  26.4 7.2 fusion.43
  33.8 0.8 constant_dynamic-update-slice_fusion.2
  34.6 7.2 fusion.43
  42.0 0.9 constant_dynamic-update-slice_fusion.2
  42.9 138.0 %all-gather.4.cloned.1.call-done = bf16[1024,4096]{1,0:T(8,128)(2,1)} async-done(((bf16[128,4096]{1,0:T(8,128)(2,1)}), bf16[1024,4096]{1,0:T(8,128)(2,1)}) %all-gather.4.cloned.1.call-update) | async-done | bytes 8388624 | tf_op jit(solution)/shard_map/all_gather | solution.py:60
  180.9 5.1 fusion.10
  186.0 10.3 %fusion.12 = bf16[1024,4096]{1,0:T(8,128)(2,1)} fusion(bf16[1024,4096]{1,0:T(8,128)(2,1)} %all-gather.4.cloned.1.call-done, f32[4096]{0:T(1024)S(1)} %copy-done.1, f32[1024]{0:T(1024)S(1)} %add_rsqrt_fusion), kind=kLoop, calls=%fused_computation.19 | loop fusion | flops 16777216 | bytes 16797696 | tf_op jit(solution)/shard_map/convert_element_type | solution.py:63
  196.3 43.5 %all-gather.6.cloned.1.call-done = bf16[4096,512]{1,0:T(8,128)(2,1)} async-done(((bf16[256,512]{1,0:T(8,128)(2,1)}), bf16[4096,512]{1,0:T(8,128)(2,1)}) %all-gather.6.cloned.1.call-update) | async-done | bytes 4194320 | tf_op jit(solution)/shard_map/all_gather | solution.py:65
  239.8 9.1 %convolution_convert_fusion.1 = bf16[1024,512]{1,0:T(8,128)(2,1)S(1)} fusion(bf16[1024,4096]{1,0:T(8,128)(2,1)} %fusion.12, bf16[4096,512]{1,0:T(8,128)(2,1)} %all-gather.6.cloned.1.call-done), kind=kOutput, calls=%fused_computation.35 | convolution fusion | flops 4295491584 | bytes 13631488 | tf_op jit(solution)/shard_map/dot_general | solution.py:66
  248.9 1.0 copy-done.3
  249.8 5.6 convolution_multiply_fusion
  255.5 78.3 %reduce-scatter.4.cloned.1.call-done = f32[256,2048]{1,0:T(8,128)} async-done(((f32[1024,2048]{1,0:T(8,128)}), f32[256,2048]{1,0:T(8,128)}) %reduce-scatter.4.cloned.1.call-update) | async-done | bytes 2097168 | tf_op jit(solution)/shard_map/reduce_scatter | solution.py:15
  333.9 0.8 dynamic-slice_subtract_fusion
  334.6 35.3 %reduce-scatter.6.cloned.1.call-done = f32[128,2048]{1,0:T(8,128)} async-done(((f32[256,2048]{1,0:T(8,128)}), f32[128,2048]{1,0:T(8,128)}) %reduce-scatter.6.cloned.1.call-update) | async-done | bytes 1048592 | tf_op jit(solution)/shard_map/reduce_scatter | solution.py:15
  369.9 1.4 reduce_max.9
  371.3 1.6 exponential_reduce_fusion
  372.9 14.4 %all_to_all.5 = f32[16,3,128]{2,1,0:T(4,128)S(1)} all-to-all(f32[16,3,128]{2,1,0:T(4,128)S(1)} %broadcast_in_dim.28), channel_id=1, replica_groups=mesh['psg'=16,'qry_0'=4,'qry_1'=2] {'psg'}, dimensions={0} | all-to-all | bytes 49152 | tf_op jit(solution)/shard_map/all_to_all | solution.py:21
  387.7 0.5 bitcast_subtract_fusion
  388.3 2.4 subtract_convert_fusion
  390.8 87.4 %all-gather.8.cloned.1.call-done = bf16[1024,2048]{1,0:T(8,128)(2,1)} async-done(((bf16[128,2048]{1,0:T(8,128)(2,1)}), bf16[1024,2048]{1,0:T(8,128)(2,1)}) %all-gather.8.cloned.1.call-update) | async-done | bytes 4194320 | tf_op jit(solution)/shard_map/all_gather | solution.py:110
  478.2 5.9 multiply_convert_fusion
  484.1 2.9 copy.19
  487.0 2.8 reshape.74
  489.8 3.3 copy.20
  493.1 35.0 %while.22 = (s32[]{:T(128)}, f32[64,8,256]{2,1,0:T(8,128)S(1)}, bf16[4,512,64,8]{1,3,2,0:T(8,128)(2,1)}, s32[4,512,64]{1,2,0:T(8,128)S(1)}, s32[]{:T(128)}, /*index=5*/s32[]{:T(128)}) while((s32[]{:T(128)}, f32[64,8,256]{2,1,0:T(8,128)S(1)}, bf16[4,512,64,8]{1,3,2,0:T(8,128)(2,1)}, s32[4,512,64]{1,2,0:T(8,128)S(1)}, s32[]{:T(128)}, ...), condition=%wide.region_13.14_spmd.clone, body=%wide.region_12.13_spmd.clone.sunk | while | flops 142868480 | bytes 1966675 | solution.py:132
  493.1 8.7 %fusion.45 = f32[64,8,256]{2,1,0:T(8,128)S(1)} fusion(s32[512,64]{0,1:T(8,128)S(1)} %dynamic-slice_bitcast_fusion.5, f32[64,8,256]{2,1,0:T(8,128)S(1)} %get-tuple-element.191, bf16[4,512,64,8]{1,3,2,0:T(8,128)(2,1)} %get-tuple-element.198, s32[]{:T(128)} %get-tuple-element.190, pred[]{:T(512)S(6)} %compare.3), kind=kOutput, calls=%fused_computation.10.clone.1 | convolution fusion | flops 142868480 | bytes 1704449 | tf_op jit(solution)/shard_map/while/body/eval_jaxpr/pmk,pmd->mdk/dot_general | solution.py:128
  501.9 8.7 %fusion.45 = f32[64,8,256]{2,1,0:T(8,128)S(1)} fusion(s32[512,64]{0,1:T(8,128)S(1)} %dynamic-slice_bitcast_fusion.5, f32[64,8,256]{2,1,0:T(8,128)S(1)} %get-tuple-element.191, bf16[4,512,64,8]{1,3,2,0:T(8,128)(2,1)} %get-tuple-element.198, s32[]{:T(128)} %get-tuple-element.190, pred[]{:T(512)S(6)} %compare.3), kind=kOutput, calls=%fused_computation.10.clone.1 | convolution fusion | flops 142868480 | bytes 1704449 | tf_op jit(solution)/shard_map/while/body/eval_jaxpr/pmk,pmd->mdk/dot_general | solution.py:128
  510.6 8.7 %fusion.45 = f32[64,8,256]{2,1,0:T(8,128)S(1)} fusion(s32[512,64]{0,1:T(8,128)S(1)} %dynamic-slice_bitcast_fusion.5, f32[64,8,256]{2,1,0:T(8,128)S(1)} %get-tuple-element.191, bf16[4,512,64,8]{1,3,2,0:T(8,128)(2,1)} %get-tuple-element.198, s32[]{:T(128)} %get-tuple-element.190, pred[]{:T(512)S(6)} %compare.3), kind=kOutput, calls=%fused_computation.10.clone.1 | convolution fusion | flops 142868480 | bytes 1704449 | tf_op jit(solution)/shard_map/while/body/eval_jaxpr/pmk,pmd->mdk/dot_general | solution.py:128
  519.4 8.7 %fusion.45 = f32[64,8,256]{2,1,0:T(8,128)S(1)} fusion(s32[512,64]{0,1:T(8,128)S(1)} %dynamic-slice_bitcast_fusion.5, f32[64,8,256]{2,1,0:T(8,128)S(1)} %get-tuple-element.191, bf16[4,512,64,8]{1,3,2,0:T(8,128)(2,1)} %get-tuple-element.198, s32[]{:T(128)} %get-tuple-element.190, pred[]{:T(512)S(6)} %compare.3), kind=kOutput, calls=%fused_computation.10.clone.1 | convolution fusion | flops 142868480 | bytes 1704449 | tf_op jit(solution)/shard_map/while/body/eval_jaxpr/pmk,pmd->mdk/dot_general | solution.py:128
  528.1 0.7 convert_element_type.58
  528.9 6.5 convolution_multiply_fusion.1
  535.4 77.4 %all-reduce.4 = bf16[1024,512]{1,0:T(8,128)(2,1)S(1)} all-reduce(f32[1024,512]{1,0:T(8,128)} %convolution_multiply_fusion.1), channel_id=1, replica_groups=mesh['psg'=16,'qry_0'=4,'qry_1'=2] {'psg'}, use_global_device_ids=true, to_apply=%region_9.10 | all-reduce | flops 524288 | bytes 3145728 | tf_op jit(solution)/shard_map/psum | solution.py:112
  612.8 8.9 %convolution_convert_fusion = bf16[1024,4096]{1,0:T(8,128)(2,1)} fusion(bf16[4096,512]{1,0:T(8,128)(2,1)} %all-gather.6.cloned.1.call-done, bf16[1024,512]{1,0:T(8,128)(2,1)S(1)} %all-reduce.4), kind=kOutput, calls=%fused_computation.20 | convolution fusion | flops 4299161600 | bytes 13631488 | tf_op jit(solution)/shard_map/dot_general | solution.py:141
  621.8 2.4 fusion.20
  624.2 44.1 %all-reduce.3.cloned.1.call-done = bf16[64,8,256]{2,1,0:T(8,128)(2,1)} async-done(((bf16[64,8,256]{2,1,0:T(8,128)(2,1)}), bf16[64,8,256]{2,1,0:T(8,128)(2,1)}) %all-reduce.3.cloned.1.call-update) | async-done | bytes 262160 | tf_op jit(solution)/shard_map/psum | solution.py:135
  668.2 1.8 convert_element_type.59
  670.0 170.9 %reduce-scatter.8.cloned.1.call-done = bf16[128,4096]{1,0:T(8,128)(2,1)} async-done(((bf16[1024,4096]{1,0:T(8,128)(2,1)}), bf16[128,4096]{1,0:T(8,128)(2,1)}) %reduce-scatter.8.cloned.1.call-update) | async-done | bytes 1048592 | tf_op jit(solution)/shard_map/reduce_scatter | solution.py:144
  840.9 1.8 fusion.13
  842.7 2.9 fusion.18
  (63 shorter events, 1.6 us)
Async XLA Ops:
  7.2 173.7 %all-gather.4.cloned.1.call-start = ((), (), s32[]{:S(2)}) async-start(), calls=%async_computation.4 | async-start | bytes 9437184 | tf_op jit(solution)/shard_map/all_gather | solution.py:60
  7.9 231.9 %all-gather.6.cloned.1.call-start = ((), (), s32[]{:S(2)}) async-start(), calls=%async_computation.5 | async-start | bytes 4456448 | tf_op jit(solution)/shard_map/all_gather | solution.py:65
  8.6 325.1 %reduce-scatter.4.cloned.1.call-start = ((), (), s32[]{:S(2)}) async-start(), calls=%async_computation.6 | async-start | bytes 10485760 | tf_op jit(solution)/shard_map/reduce_scatter | solution.py:15
  42.9 143.1 %copy-start.1 = (f32[4096]{0:T(1024)S(1)}, f32[4096]{0:T(1024)}, u32[]{:S(2)}) copy-start(f32[4096]{0:T(1024)} %param.11) | copy-start | bytes 49156
  196.3 53.5 %copy-start.2 = (bf16[4,512,512]{2,1,0:T(8,128)(2,1)S(1)}, bf16[4,512,512]{2,1,0:T(8,128)(2,1)}, u32[]{:S(2)}) copy-start(bf16[4,512,512]{2,1,0:T(8,128)(2,1)} %get-tuple-element.48) | copy-start | bytes 6291460
  248.9 1.0 copy-start.3
  255.5 222.7 %copy-start.4 = (bf16[1024,512]{1,0:T(8,128)(2,1)S(1)}, bf16[1024,512]{1,0:T(8,128)(2,1)}, u32[]{:S(2)}) copy-start(bf16[1024,512]{1,0:T(8,128)(2,1)} %copy-done.3) | copy-start | bytes 3145732
  255.5 114.4 %reduce-scatter.6.cloned.1.call-start = ((), (), s32[]{:S(2)}) async-start(), calls=%async_computation.7 | async-start | bytes 3145728 | tf_op jit(solution)/shard_map/reduce_scatter | solution.py:15
  333.8 144.4 %all-gather.8.cloned.1.call-start = ((), (), s32[]{:S(2)}) async-start(), calls=%async_computation.8 | async-start | bytes 4718592 | tf_op jit(solution)/shard_map/all_gather | solution.py:110
  390.7 277.5 %all-reduce.3.cloned.1.call-start = ((), (), s32[]{:S(2)}) async-start(), calls=%async_computation.10 | async-start | bytes 524288 | tf_op jit(solution)/shard_map/psum | solution.py:135
  528.9 312.1 %reduce-scatter.8.cloned.1.call-start = ((), (), s32[]{:S(2)}) async-start(), calls=%async_computation.9 | async-start | bytes 9437184 | tf_op jit(solution)/shard_map/reduce_scatter | solution.py:144
  621.8 219.2 %copy-start = (bf16[128,4096]{1,0:T(8,128)(2,1)S(1)}, bf16[128,4096]{1,0:T(8,128)(2,1)}, u32[]{:S(2)}) copy-start(bf16[128,4096]{1,0:T(8,128)(2,1)} %param.10) | copy-start | bytes 3145732
Sparse Core Ops, SparseCore 0:
  9.6 171.2 all-gather.3
  183.4 56.3 all-gather.5
  255.6 78.1 reduce-scatter.3
  336.0 33.8 reduce-scatter.5
  390.9 87.2 all-gather.7
  529.0 139.1 all-reduce.2
  670.6 170.2 reduce-scatter.7
where the time goes:
time: 854 us; the launch traced here: 852 us
  waiting for transfers between devices  599 us (70%)
  matrix products  102 us (12%)
  blocking collectives  91.8 us (11%)
  other arithmetic  29.4 us (3%)
  local copies, waits for them, and re-layouts  15.8 us (2%)
  between operations  14.3 us (2%)
    reduce_scatter x1, waiting for transfers between devices, per_device(): lax.psum_scatter(norm_part.astype(jnp.bfloat16), QRY, scatter_dimension=0...  171 us
    all_gather x1, waiting for transfers between devices, per_device(): gathered = lax.all_gather(hidden, QRY, axis=0, tiled=True)  138 us
    reduce_scatter x2, waiting for transfers between devices, summed_rows(): nearer = lax.psum_scatter(x, axes[0], scatter_dimension=dim, tiled=True)  114 us
    all_gather x1, waiting for transfers between devices, per_device(): all_grad = lax.all_gather(score_grad, QRY, axis=0, tiled=True)  87.4 us
    psum x1, blocking collectives, per_device(): query_grad = lax.psum(query_part, 'psg').astype(jnp.bfloat16)  77.4 us
    psum x1, waiting for transfers between devices, per_device(): lax.psum(book_part.astype(jnp.bfloat16), 'psg').astype(jnp.float32)  44.1 us
    all_gather x1, waiting for transfers between devices, per_device(): whole_weight = lax.all_gather(proj_weight, 'psg', axis=0, tiled=True)  43.5 us
    dot_general x4, matrix products, add_book(): jnp.einsum('pmk,pmd->mdk', hot_table, grad_block, preferred_element_type=...  34.9 us
  transfers between devices with their start and end apart: 7, of which 7 were waited for; matrix products, arithmetic and copies ran while one was open for 8% of the time, Pallas kernels for 0%

commit v1 on v0

--- a/solution.py
+++ b/solution.py
@@ -109,7 +109,7 @@
     ).astype(jnp.bfloat16)
     all_grad = lax.all_gather(score_grad, QRY, axis=0, tiled=True)
     query_part = jnp.dot(all_grad, passages, preferred_element_type=jnp.float32) * score_scale
-    query_grad = lax.psum(query_part, "psg").astype(jnp.bfloat16)
+    query_grad = jnp.sum(lax.all_gather(query_part, "psg"), axis=0).astype(jnp.bfloat16)
     passage_grad = (
         lax.dot_general(
             all_grad, queries, (((0,), (0,)), ((), ())), preferred_element_type=jnp.float32

time: 854 us -> 995 us (1.17)
  waiting for transfers between devices: 599 us -> 797 us
  blocking collectives: 91.8 us -> 14.4 us
  other arithmetic: 29.4 us -> 42.2 us
    all_gather x0 -> x1, waiting for transfers between devices: none -> 127 us  [per_device(): lax.all_gather(query_part, 'psg')]
    psum x1 -> x0, blocking collectives: 77.4 us -> none  [per_device(): query_grad = lax.psum(query_part, 'psg').astype(jnp.bfloat16)]
    psum x1, waiting for transfers between devices: 44.1 us -> 117 us  [per_device(): lax.psum(book_part.astype(jnp.bfloat16), 'psg').astype(jnp.float32)]
    reduce_sum x0 -> x1, other arithmetic: none -> 12.8 us  [per_device(): jnp.sum(lax.all_gather(query_part, 'psg'), axis=0).astype(jnp.bfloat16)]
  transfers between devices with their start and end apart: 7 -> 8, of which waited for: 7 -> 8; matrix products, arithmetic and copies ran while one was open for 8% -> 14% of each run, Pallas kernels for 0% -> 0%
where the time goes in v1:
time: 995 us; the launch traced here: 994 us
  waiting for transfers between devices  797 us (80%)
  matrix products  111 us (11%)
  other arithmetic  42.2 us (4%)
  local copies, waits for them, and re-layouts  14.7 us (1%)
  blocking collectives  14.4 us (1%)
  between operations  14.3 us (1%)
    reduce_scatter x1, waiting for transfers between devices, per_device(): lax.psum_scatter(norm_part.astype(jnp.bfloat16), QRY, scatter_dimension=0...  169 us
    all_gather x1, waiting for transfers between devices, per_device(): gathered = lax.all_gather(hidden, QRY, axis=0, tiled=True)  138 us
    all_gather x1, waiting for transfers between devices, per_device(): lax.all_gather(query_part, 'psg')  127 us
    psum x1, waiting for transfers between devices, per_device(): lax.psum(book_part.astype(jnp.bfloat16), 'psg').astype(jnp.float32)  117 us
    reduce_scatter x2, waiting for transfers between devices, summed_rows(): nearer = lax.psum_scatter(x, axes[0], scatter_dimension=dim, tiled=True)  114 us
    all_gather x1, waiting for transfers between devices, per_device(): all_grad = lax.all_gather(score_grad, QRY, axis=0, tiled=True)  87.4 us
    dot_general x4, matrix products, add_book(): jnp.einsum('pmk,pmd->mdk', hot_table, grad_block, preferred_element_type=...  44 us
    all_gather x1, waiting for transfers between devices, per_device(): whole_weight = lax.all_gather(proj_weight, 'psg', axis=0, tiled=True)  43.4 us
  transfers between devices with their start and end apart: 8, of which 8 were waited for; matrix products, arithmetic and copies ran while one was open for 14% of the time, Pallas kernels for 0%

profile of v1, /device:TPU:1, one launch (start us, length us, event | category | flops | bytes accessed | tf_op | source)
XLA Modules:
  0.0 993.5 jit_solution(10880669878259769187)
XLA Ops:
  7.2 0.7 all-gather.6.cloned.1.call-update
  7.9 0.7 all-gather.8.cloned.1.call-update
  8.7 1.1 copy.27
  9.8 33.1 %while.21 = (s32[]{:T(128)}, bf16[4,512,512]{2,1,0:T(8,128)(2,1)}, s32[4,512,64]{1,2,0:T(8,128)S(1)}, bf16[64,8,256]{2,1,0:T(8,128)(2,1)}, s32[]{:T(128)}) while((s32[]{:T(128)}, bf16[4,512,512]{2,1,0:T(8,128)(2,1)}, s32[4,512,64]{1,2,0:T(8,128)S(1)}, bf16[64,8,256]{2,1,0:T(8,128)(2,1)}, s32[]{:T(128)}) %tuple.76), condition=%wide.region_2.3_spmd, body=%wide.region_1.2_spmd.sunk | while | flops 142868480 | bytes 3276877 | solution.py:81
  9.8 7.2 fusion.43
  17.2 0.9 constant_dynamic-update-slice_fusion.2
  18.1 7.2 fusion.43
  25.6 0.9 constant_dynamic-update-slice_fusion.2
  26.4 7.2 fusion.43
  33.9 0.8 constant_dynamic-update-slice_fusion.2
  34.7 7.2 fusion.43
  42.1 0.8 constant_dynamic-update-slice_fusion.2
  42.9 138.1 %all-gather.6.cloned.1.call-done = bf16[1024,4096]{1,0:T(8,128)(2,1)} async-done(((bf16[128,4096]{1,0:T(8,128)(2,1)}), bf16[1024,4096]{1,0:T(8,128)(2,1)}) %all-gather.6.cloned.1.call-update) | async-done | bytes 8388624 | tf_op jit(solution)/shard_map/all_gather | solution.py:60
  181.0 5.1 fusion.10
  186.1 10.3 %fusion.12 = bf16[1024,4096]{1,0:T(8,128)(2,1)} fusion(bf16[1024,4096]{1,0:T(8,128)(2,1)} %all-gather.6.cloned.1.call-done, f32[4096]{0:T(1024)S(1)} %copy-done.1, f32[1024]{0:T(1024)S(1)} %add_rsqrt_fusion), kind=kLoop, calls=%fused_computation.19 | loop fusion | flops 16777216 | bytes 16797696 | tf_op jit(solution)/shard_map/convert_element_type | solution.py:63
  196.4 43.4 %all-gather.8.cloned.1.call-done = bf16[4096,512]{1,0:T(8,128)(2,1)} async-done(((bf16[256,512]{1,0:T(8,128)(2,1)}), bf16[4096,512]{1,0:T(8,128)(2,1)}) %all-gather.8.cloned.1.call-update) | async-done | bytes 4194320 | tf_op jit(solution)/shard_map/all_gather | solution.py:65
  239.8 9.0 convolution_convert_fusion.1
  248.9 1.0 copy-done.3
  249.8 5.6 convolution_multiply_fusion
  255.5 78.3 %reduce-scatter.4.cloned.1.call-done = f32[256,2048]{1,0:T(8,128)} async-done(((f32[1024,2048]{1,0:T(8,128)}), f32[256,2048]{1,0:T(8,128)}) %reduce-scatter.4.cloned.1.call-update) | async-done | bytes 2097168 | tf_op jit(solution)/shard_map/reduce_scatter | solution.py:15
  333.9 0.8 dynamic-slice_subtract_fusion
  334.6 35.3 %reduce-scatter.6.cloned.1.call-done = f32[128,2048]{1,0:T(8,128)} async-done(((f32[256,2048]{1,0:T(8,128)}), f32[128,2048]{1,0:T(8,128)}) %reduce-scatter.6.cloned.1.call-update) | async-done | bytes 1048592 | tf_op jit(solution)/shard_map/reduce_scatter | solution.py:15
  369.9 1.4 reduce_max.9
  371.2 1.6 exponential_reduce_fusion
  372.9 14.4 %all_to_all.5 = f32[16,3,128]{2,1,0:T(4,128)S(1)} all-to-all(f32[16,3,128]{2,1,0:T(4,128)S(1)} %broadcast_in_dim.28), channel_id=1, replica_groups=mesh['psg'=16,'qry_0'=4,'qry_1'=2] {'psg'}, dimensions={0} | all-to-all | bytes 49152 | tf_op jit(solution)/shard_map/all_to_all | solution.py:21
  387.7 0.5 bitcast_subtract_fusion
  388.2 2.4 subtract_convert_fusion
  390.8 87.4 %all-gather.10.cloned.1.call-done = bf16[1024,2048]{1,0:T(8,128)(2,1)} async-done(((bf16[128,2048]{1,0:T(8,128)(2,1)}), bf16[1024,2048]{1,0:T(8,128)(2,1)}) %all-gather.10.cloned.1.call-update) | async-done | bytes 4194320 | tf_op jit(solution)/shard_map/all_gather | solution.py:110
  478.1 5.8 convolution_multiply_fusion.1
  484.1 6.2 multiply_convert_fusion
  490.3 2.9 copy.19
  493.2 2.8 reshape.74
  496.0 2.3 copy.20
  498.3 44.1 %while.22 = (s32[]{:T(128)}, f32[64,8,256]{2,1,0:T(8,128)S(1)}, bf16[4,512,64,8]{1,3,2,0:T(8,128)(2,1)S(1)}, s32[4,512,64]{1,2,0:T(8,128)S(1)}, s32[]{:T(128)}, /*index=5*/s32[]{:T(128)}) while((s32[]{:T(128)}, f32[64,8,256]{2,1,0:T(8,128)S(1)}, bf16[4,512,64,8]{1,3,2,0:T(8,128)(2,1)S(1)}, s32[4,512,64]{1,2,0:T(8,128)S(1)}, ...), condition=%wide.region_13.14_spmd.clone, body=%wide.region_12.13_spmd.clone.sunk | while | flops 142868480 | bytes 1966175 | solution.py:132
  498.3 11.0 %fusion.45 = f32[64,8,256]{2,1,0:T(8,128)S(1)} fusion(s32[512,64]{0,1:T(8,128)S(1)} %dynamic-slice_bitcast_fusion.5, f32[64,8,256]{2,1,0:T(8,128)S(1)} %get-tuple-element.191, bf16[4,512,64,8]{1,3,2,0:T(8,128)(2,1)S(1)} %get-tuple-element.198, s32[]{:T(128)S(6)} %copy.39, pred[]{:T(512)S(6)} %compare.3), kind=kOutput, calls=%fused_computation.10.clone.1 | convolution fusion | flops 142868480 | bytes 1703941 | tf_op jit(solution)/shard_map/while/body/eval_jaxpr/pmk,pmd->mdk/dot_general | solution.py:128
  509.3 11.0 %fusion.45 = f32[64,8,256]{2,1,0:T(8,128)S(1)} fusion(s32[512,64]{0,1:T(8,128)S(1)} %dynamic-slice_bitcast_fusion.5, f32[64,8,256]{2,1,0:T(8,128)S(1)} %get-tuple-element.191, bf16[4,512,64,8]{1,3,2,0:T(8,128)(2,1)S(1)} %get-tuple-element.198, s32[]{:T(128)S(6)} %copy.39, pred[]{:T(512)S(6)} %compare.3), kind=kOutput, calls=%fused_computation.10.clone.1 | convolution fusion | flops 142868480 | bytes 1703941 | tf_op jit(solution)/shard_map/while/body/eval_jaxpr/pmk,pmd->mdk/dot_general | solution.py:128
  520.3 11.0 %fusion.45 = f32[64,8,256]{2,1,0:T(8,128)S(1)} fusion(s32[512,64]{0,1:T(8,128)S(1)} %dynamic-slice_bitcast_fusion.5, f32[64,8,256]{2,1,0:T(8,128)S(1)} %get-tuple-element.191, bf16[4,512,64,8]{1,3,2,0:T(8,128)(2,1)S(1)} %get-tuple-element.198, s32[]{:T(128)S(6)} %copy.39, pred[]{:T(512)S(6)} %compare.3), kind=kOutput, calls=%fused_computation.10.clone.1 | convolution fusion | flops 142868480 | bytes 1703941 | tf_op jit(solution)/shard_map/while/body/eval_jaxpr/pmk,pmd->mdk/dot_general | solution.py:128
  531.4 11.0 %fusion.45 = f32[64,8,256]{2,1,0:T(8,128)S(1)} fusion(s32[512,64]{0,1:T(8,128)S(1)} %dynamic-slice_bitcast_fusion.5, f32[64,8,256]{2,1,0:T(8,128)S(1)} %get-tuple-element.191, bf16[4,512,64,8]{1,3,2,0:T(8,128)(2,1)S(1)} %get-tuple-element.198, s32[]{:T(128)S(6)} %copy.39, pred[]{:T(512)S(6)} %compare.3), kind=kOutput, calls=%fused_computation.10.clone.1 | convolution fusion | flops 142868480 | bytes 1703941 | tf_op jit(solution)/shard_map/while/body/eval_jaxpr/pmk,pmd->mdk/dot_general | solution.py:128
  542.4 0.7 convert_element_type.58
  543.2 127.0 %all-gather.12.cloned.1.call-done = f32[16384,512]{1,0:T(8,128)} async-done(((f32[1024,512]{1,0:T(8,128)}), f32[16384,512]{1,0:T(8,128)}) %all-gather.12.cloned.1.call-update) | async-done | bytes 33554448 | tf_op jit(solution)/shard_map/all_gather | solution.py:112
  670.2 12.8 %reduce_sum.58 = bf16[1024,512]{1,0:T(8,128)(2,1)S(1)} reduce(f32[16,1024,512]{2,1,0:T(8,128)} %bitcast.57, f32[]{:T(128)} %constant.17.clone.1), dimensions={0}, to_apply=%region_9.10 | reduce | flops 7864320 | bytes 34603012 | tf_op jit(solution)/shard_map/reduce_sum | solution.py:112
  683.0 9.0 convolution_convert_fusion
  692.0 117.2 %all-reduce.2.cloned.1.call-done = bf16[64,8,256]{2,1,0:T(8,128)(2,1)} async-done(((bf16[64,8,256]{2,1,0:T(8,128)(2,1)}), bf16[64,8,256]{2,1,0:T(8,128)(2,1)}) %all-reduce.2.cloned.1.call-update) | async-done | bytes 262160 | tf_op jit(solution)/shard_map/psum | solution.py:135
  809.2 1.8 convert_element_type.59
  811.0 2.3 fusion.20
  813.3 168.6 %reduce-scatter.8.cloned.1.call-done = bf16[128,4096]{1,0:T(8,128)(2,1)} async-done(((bf16[1024,4096]{1,0:T(8,128)(2,1)}), bf16[128,4096]{1,0:T(8,128)(2,1)}) %reduce-scatter.8.cloned.1.call-update) | async-done | bytes 1048592 | tf_op jit(solution)/shard_map/reduce_scatter | solution.py:144
  981.9 1.8 fusion.13
  983.7 2.9 fusion.18
  (64 shorter events, 1.8 us)
Async XLA Ops:
  7.2 173.8 %all-gather.6.cloned.1.call-start = ((), (), s32[]{:S(2)}) async-start(), calls=%async_computation.4 | async-start | bytes 9437184 | tf_op jit(solution)/shard_map/all_gather | solution.py:60
  7.9 231.9 %all-gather.8.cloned.1.call-start = ((), (), s32[]{:S(2)}) async-start(), calls=%async_computation.5 | async-start | bytes 4456448 | tf_op jit(solution)/shard_map/all_gather | solution.py:65
  8.6 325.1 %reduce-scatter.4.cloned.1.call-start = ((), (), s32[]{:S(2)}) async-start(), calls=%async_computation.6 | async-start | bytes 10485760 | tf_op jit(solution)/shard_map/reduce_scatter | solution.py:15
  42.9 143.2 %copy-start.1 = (f32[4096]{0:T(1024)S(1)}, f32[4096]{0:T(1024)}, u32[]{:S(2)}) copy-start(f32[4096]{0:T(1024)} %param.11) | copy-start | bytes 49156
  196.4 53.4 %copy-start.2 = (bf16[4,512,512]{2,1,0:T(8,128)(2,1)S(1)}, bf16[4,512,512]{2,1,0:T(8,128)(2,1)}, u32[]{:S(2)}) copy-start(bf16[4,512,512]{2,1,0:T(8,128)(2,1)} %get-tuple-element.48) | copy-start | bytes 6291460
  248.8 1.0 copy-start.3
  255.4 114.4 %reduce-scatter.6.cloned.1.call-start = ((), (), s32[]{:S(2)}) async-start(), calls=%async_computation.7 | async-start | bytes 3145728 | tf_op jit(solution)/shard_map/reduce_scatter | solution.py:15
  333.8 144.3 %all-gather.10.cloned.1.call-start = ((), (), s32[]{:S(2)}) async-start(), calls=%async_computation.8 | async-start | bytes 4718592 | tf_op jit(solution)/shard_map/all_gather | solution.py:110
  390.7 279.5 %all-gather.12.cloned.1.call-start = ((), (), s32[]{:S(2)}) async-start(), calls=%async_computation.11 | async-start | bytes 35651584 | tf_op jit(solution)/shard_map/all_gather | solution.py:112
  484.0 325.2 %all-reduce.2.cloned.1.call-start = ((), (), s32[]{:S(2)}) async-start(), calls=%async_computation.10 | async-start | bytes 524288 | tf_op jit(solution)/shard_map/psum | solution.py:135
  543.1 438.8 %reduce-scatter.8.cloned.1.call-start = ((), (), s32[]{:S(2)}) async-start(), calls=%async_computation.9 | async-start | bytes 9437184 | tf_op jit(solution)/shard_map/reduce_scatter | solution.py:144
  692.0 290.0 %copy-start = (bf16[128,4096]{1,0:T(8,128)(2,1)S(1)}, bf16[128,4096]{1,0:T(8,128)(2,1)}, u32[]{:S(2)}) copy-start(bf16[128,4096]{1,0:T(8,128)(2,1)} %param.10) | copy-start | bytes 3145732
Sparse Core Ops, SparseCore 0:
  9.6 171.3 all-gather.5
  183.5 56.2 all-gather.7
  255.6 78.1 reduce-scatter.3
  336.0 33.8 reduce-scatter.5
  390.8 87.2 all-gather.9
  484.1 186.0 all-gather.11
  673.2 135.9 all-reduce.1
  811.6 170.2 reduce-scatter.7
